TPU v7x, 32 devices: a whole 2x2x4 slice. The times are simulated.
32 devices in a mesh: section: 4 (over x, core), dp: 8 (over z, y).
Axes of the slice: x: 2, y: 2, z: 4, core: 2. Of those that a mesh axis runs over, the one named last changes fastest.
Arguments:
- clean_latent: float32 [64, 256], P('dp'), may hold values from -6 to 6
- noise_draw: float32 [64, 256], P('dp'), may hold values from -6 to 6
- step_index: int32 [64], P('dp'), may hold values from 250 to 1000
- labels: int32 [64], P('dp'), may hold values from 0 to 999
- guide_level: int32 [64], P('dp'), may hold values from 0 to 8
- class_table: bfloat16 [1001, 1152], replicated, may hold values from -6 to 6
- embed_in: bfloat16 [16, 1152], replicated, may hold values from -1.5 to 1.5
- embed_out: bfloat16 [1152, 16], replicated, may hold values from -0.1875 to 0.1875
- teacher_up: bfloat16 [4, 1152, 2304], P('section', 'dp'), may hold values from -0.1875 to 0.1875
- teacher_down: bfloat16 [4, 2304, 1152], P('section', 'dp'), may hold values from -0.125 to 0.125
- teacher_gain: float32 [4, 3, 1152], P('section'), may hold values from -3 to 3
- teacher_bias: float32 [4, 3, 1152], P('section'), may hold values from -3 to 3
- student_up: bfloat16 [1152, 4608], P(None, 'section'), may hold values from -0.1875 to 0.1875
- student_down: bfloat16 [4608, 1152], P('section'), may hold values from -0.09375 to 0.09375
- student_gain: float32 [3, 1152], replicated, may hold values from -3 to 3
- student_bias: float32 [3, 1152], replicated, may hold values from -3 to 3
- guide_vec: float32 [1152], replicated, may hold values from -3 to 3
Outputs:
- distill_target: float32 [64, 256], P('dp')
- grad_up: float32 [1152, 4608], P('dp', 'section')
- grad_down: float32 [4608, 1152], P(('section', 'dp'))
All inputs are finite; a program needn't handle non-finite values.
Results may differ from a plain program's by a relative error of at most 0.017.
Values may be sent and summed in bfloat16 or wider, within the bound.
A program may use at most 128 MiB of HBM per device.

v0:
```python
import math

import jax
import jax.numpy as jnp
from jax import lax
from jax.sharding import PartitionSpec as P

CH = 16
TSTEPS = 1000
STRIDE = 125


norm_eps = 1e-06


def shifted(shard, axis, by):
    length = lax.axis_size(axis)
    return lax.ppermute(shard, axis, [(i, (i + by) % length) for i in range(length)])


def from_root(shard, axis, root):
    mine = lax.axis_index(axis) == root
    return lax.psum(jnp.where(mine, shard, jnp.zeros_like(shard)), axis)


def layer_norm(values):
    center = values - jnp.mean(values, axis=-1, keepdims=True)
    spread = jnp.mean(center * center, axis=-1, keepdims=True)
    return center * lax.rsqrt(spread + norm_eps)


def sinusoid(step_ids, model_width):
    half_width = model_width // 2
    frequency = jnp.exp(-math.log(10000.0) * jnp.arange(half_width, dtype=jnp.float32) / half_width)
    phase_arg = step_ids.astype(jnp.float32)[:, None] * frequency[None, :]
    return jnp.concatenate([jnp.cos(phase_arg), jnp.sin(phase_arg)], axis=-1)


def plan(step_ids):
    angle_t = 0.5 * math.pi / TSTEPS * step_ids.astype(jnp.float32)
    return (jnp.cos(angle_t), jnp.sin(angle_t))


def embed_tokens(latent, embed_in):
    leading = latent.shape[0]
    patches = latent.reshape(leading * (latent.shape[1] // CH), CH).astype(jnp.bfloat16)
    tokens = jnp.dot(patches, embed_in, preferred_element_type=jnp.float32)
    return tokens.reshape(leading, latent.shape[1] // CH, embed_in.shape[1]).astype(jnp.bfloat16)


def mlp_block(inputs, modulation, up_proj, down_proj):
    groups, seq_len, model_width = inputs.shape
    residual_in = inputs.astype(jnp.float32)
    shift_rows = modulation[:, 0, None, :]
    scale_rows = modulation[:, 1, None, :]
    gate_rows = modulation[:, 2, None, :]
    normed = (layer_norm(residual_in) * (1.0 + scale_rows) + shift_rows).astype(jnp.bfloat16)
    pre_act = jnp.dot(
        normed.reshape(groups * seq_len, model_width), up_proj, preferred_element_type=jnp.float32
    )
    hidden = jax.nn.gelu(pre_act, approximate=True).astype(jnp.bfloat16)
    mixed = jnp.dot(hidden, down_proj, preferred_element_type=jnp.float32).reshape(
        groups, seq_len, model_width
    )
    return (residual_in + gate_rows * mixed).astype(jnp.bfloat16)


def velocity(states, embed_out):
    groups, seq_len, model_width = states.shape
    normed = layer_norm(states.astype(jnp.float32)).astype(jnp.bfloat16)
    result = jnp.dot(
        normed.reshape(groups * seq_len, model_width), embed_out, preferred_element_type=jnp.float32
    )
    return result.reshape(groups, seq_len * embed_out.shape[1])


def ddim_step(latent, predicted, time_now, time_next):
    alpha_now, sigma_now = plan(time_now)
    alpha_next, sigma_next = plan(time_next)
    clean_est = alpha_now[:, None] * latent - sigma_now[:, None] * predicted
    noise_est = sigma_now[:, None] * latent + alpha_now[:, None] * predicted
    return alpha_next[:, None] * clean_est + sigma_next[:, None] * noise_est


def gelu_slope(pre_act):
    return jax.vjp(lambda inner: jax.nn.gelu(inner, approximate=True), pre_act)[1](
        jnp.ones_like(pre_act)
    )[0]


def record(buffer, sample_at, values, write_flag):
    current = lax.dynamic_index_in_dim(buffer, sample_at, 0, keepdims=False)
    return lax.dynamic_update_index_in_dim(
        buffer, jnp.where(write_flag, values, current), sample_at, 0
    )


def body(
    clean_latent,
    noise_draw,
    step_index,
    labels,
    guide_level,
    class_table,
    embed_in,
    embed_out,
    teacher_up,
    teacher_down,
    teacher_gain,
    teacher_bias,
    student_up,
    student_down,
    student_gain,
    student_bias,
    guide_vec,
):
    section_count = lax.axis_size("section")
    section_at = lax.axis_index("section")
    tail_section = section_count - 1
    micro_count = clean_latent.shape[0]
    seq_len = clean_latent.shape[1] // CH
    model_width = class_table.shape[1]
    teach_up, teach_down = (
        lax.all_gather(teacher_up[0], "dp", axis=0, tiled=True),
        lax.all_gather(teacher_down[0], "dp", axis=0, tiled=True),
    )
    alpha_t, sigma_t = plan(step_index)
    noised = alpha_t[:, None] * clean_latent + sigma_t[:, None] * noise_draw
    guidance = 0.5 * guide_level.astype(jnp.float32)
    label_rows = jnp.take(class_table, labels, axis=0).astype(jnp.float32)
    null_row = class_table[class_table.shape[0] - 1].astype(jnp.float32)
    wave_rows = jnp.stack(
        [sinusoid(step_index - step_k * STRIDE, model_width) for step_k in range(2)]
    )
    conditions = jnp.stack(
        [wave_rows + label_rows[None], wave_rows + null_row[None, None, :]], axis=2
    )
    teacher_mods = (
        conditions[:, :, :, None, :] * teacher_gain[0][None, None, None]
        + teacher_bias[0][None, None, None]
    )
    first_in = embed_tokens(noised, embed_in)
    pair_shape = (2, seq_len, model_width)

    def run_section(which_step, sample_at, incoming, returned, middle):
        own_input = jnp.where(which_step == 0, first_in[sample_at], returned[sample_at])
        entry_rows = jnp.where(
            section_at == 0, jnp.broadcast_to(own_input[None], pair_shape), incoming
        )
        section_out = mlp_block(
            entry_rows, teacher_mods[which_step, sample_at], teach_up, teach_down
        )
        predicted = velocity(section_out, embed_out)
        weight_now = guidance[sample_at]
        guided = (1.0 + weight_now) * predicted[0] - weight_now * predicted[1]
        time_now = step_index[sample_at] - which_step * STRIDE
        latent = jnp.where(which_step == 0, noised[sample_at], middle[sample_at])
        stepped = ddim_step(latent[None], guided[None], time_now[None], (time_now - STRIDE)[None])[
            0
        ]
        reembedded = embed_tokens(stepped[None], embed_in)[0]
        payload = jnp.where(
            section_at == tail_section, jnp.broadcast_to(reembedded[None], pair_shape), section_out
        )
        return (payload, stepped, reembedded)

    empty_pair = jnp.zeros(pair_shape, jnp.bfloat16)
    empty_latent = jnp.zeros(clean_latent.shape, jnp.float32)
    empty_tokens = jnp.zeros((micro_count, seq_len, model_width), jnp.bfloat16)

    def advance(tick_count, state_tuple):
        incoming, middle, ending, returned = state_tuple
        position = tick_count - section_at
        active = (position >= 0) & (position < 2 * micro_count)
        safe_pos = jnp.clip(position, 0, 2 * micro_count - 1)
        which_step = safe_pos // micro_count
        sample_at = safe_pos % micro_count
        payload, stepped, reembedded = run_section(
            which_step, sample_at, incoming, returned, middle
        )
        at_tail = active & (section_at == tail_section)
        middle = record(middle, sample_at, stepped, at_tail & (which_step == 0))
        ending = record(ending, sample_at, stepped, at_tail & (which_step == 1))
        incoming = shifted(payload, "section", 1)
        back_pos = tick_count - tail_section
        store_now = (section_at == 0) & (back_pos >= 0) & (back_pos < micro_count)
        slot_at = jnp.clip(back_pos, 0, micro_count - 1)
        returned = record(returned, slot_at, incoming[0], store_now)
        return (incoming, middle, ending, returned)

    start_tuple = (empty_pair, empty_latent, empty_latent, empty_tokens)
    _, middle, ending, returned = lax.fori_loop(
        0, 2 * micro_count + section_count - 1, advance, start_tuple
    )
    alpha_end, sigma_end = plan(step_index - 2 * STRIDE)
    sigma_ratio = sigma_end / sigma_t
    goal_latent = (ending - sigma_ratio[:, None] * noised) / (alpha_end - sigma_ratio * alpha_t)[
        :, None
    ]
    distill_target = from_root(goal_latent, "section", tail_section)
    student_cond = wave_rows[0] + label_rows + guidance[:, None] * guide_vec[None, :]
    modulation = student_cond[:, None, :] * student_gain[None] + student_bias[None]
    shift_rows = modulation[:, 0, None, :]
    scale_rows = modulation[:, 1, None, :]
    gate_rows = modulation[:, 2, None, :]
    row_count = micro_count * seq_len
    residual_in = first_in.astype(jnp.float32)
    normed = (
        (layer_norm(residual_in) * (1.0 + scale_rows) + shift_rows)
        .astype(jnp.bfloat16)
        .reshape(row_count, model_width)
    )
    pre_act = jnp.dot(normed, student_up, preferred_element_type=jnp.float32)
    hidden = jax.nn.gelu(pre_act, approximate=True).astype(jnp.bfloat16)
    partial_value = jnp.dot(hidden, student_down, preferred_element_type=jnp.float32)
    mixed = (
        lax.psum(partial_value.astype(jnp.bfloat16), "section")
        .astype(jnp.float32)
        .reshape(micro_count, seq_len, model_width)
    )
    state_rows = residual_in + gate_rows * mixed
    normed_out, pullback = jax.vjp(layer_norm, state_rows)
    predicted = jnp.dot(
        normed_out.astype(jnp.bfloat16).reshape(row_count, model_width),
        embed_out,
        preferred_element_type=jnp.float32,
    ).reshape(micro_count, seq_len * CH)
    estimate = alpha_t[:, None] * noised - sigma_t[:, None] * predicted
    weight = jnp.maximum(alpha_t * alpha_t / (sigma_t * sigma_t), 1.0)
    element_count = micro_count * lax.axis_size("dp") * clean_latent.shape[1]
    slope_pred = -2.0 / element_count * (sigma_t * weight)[:, None] * (estimate - distill_target)
    back_norm = jnp.dot(
        slope_pred.reshape(row_count, CH),
        embed_out.astype(jnp.float32).T,
        precision=lax.Precision.HIGHEST,
    )
    back_state = pullback(back_norm.reshape(micro_count, seq_len, model_width))[0]
    back_part = (gate_rows * back_state).astype(jnp.bfloat16).reshape(row_count, model_width)
    contract_rows = (((0,), (0,)), ((), ()))
    back_hidden = lax.dot_general(
        back_part, student_down, (((1,), (1,)), ((), ())), preferred_element_type=jnp.float32
    )
    back_pre = (back_hidden * gelu_slope(pre_act)).astype(jnp.bfloat16)
    local_up = lax.dot_general(normed, back_pre, contract_rows, preferred_element_type=jnp.float32)
    local_down = lax.dot_general(
        hidden, back_part, contract_rows, preferred_element_type=jnp.float32
    )
    grad_up, grad_down = (
        lax.psum_scatter(local_up, "dp", scatter_dimension=0, tiled=True),
        lax.psum_scatter(local_down, "dp", scatter_dimension=0, tiled=True),
    )
    return (distill_target, grad_up, grad_down)


def solution(mesh):
    return jax.shard_map(
        body,
        mesh=mesh,
        in_specs=(
            P("dp", None),
            P("dp", None),
            P("dp"),
            P("dp"),
            P("dp"),
            P(),
            P(),
            P(),
            P("section", "dp", None),
            P("section", "dp", None),
            P("section", None, None),
            P("section", None, None),
            P(None, "section"),
            P("section", None),
            P(),
            P(),
            P(),
        ),
        out_specs=(P("dp", None), P("dp", "section"), P(("section", "dp"), None)),
        check_vma=False,
    )
```

profile of v0, /device:TPU:0, one launch (start us, length us, event | category | flops | bytes accessed | tf_op | source)
XLA Modules:
  0.0 800.4 jit_solution(9463580022502839689)
XLA Ops:
  13.1 2.5 gather_fusion
  27.6 32.1 %all-reduce.2.cloned.1.call-done = bf16[8,16,1152]{2,1,0:T(8,128)(2,1)} async-done(((bf16[8,16,1152]{2,1,0:T(8,128)(2,1)}), bf16[8,16,1152]{2,1,0:T(8,128)(2,1)}) %all-reduce.2.cloned.1.call-update) | async-done | bytes 294928 | tf_op jit(solution)/shard_map/psum | solution.py:217
  64.1 52.2 %all-gather.5.cloned.1.call-done = bf16[1,1152,2304]{2,1,0:T(8,128)(2,1)} async-done(((bf16[1,144,2304]{2,1,0:T(8,128)(2,1)}), bf16[1,1152,2304]{2,1,0:T(8,128)(2,1)}) %all-gather.5.cloned.1.call-update) | async-done | bytes 5308432 | tf_op jit(solution)/shard_map/all_gather | solution.py:124
  116.3 86.8 %all-gather.7.cloned.1.call-done = bf16[1,2304,1152]{2,1,0:T(8,128)(2,1)} async-done(((bf16[1,288,1152]{2,1,0:T(8,128)(2,1)}), bf16[1,2304,1152]{2,1,0:T(8,128)(2,1)}) %all-gather.7.cloned.1.call-update) | async-done | bytes 5308432 | tf_op jit(solution)/shard_map/all_gather | solution.py:125
  204.4 355.4 %while.21 = (s32[]{:T(128)}, bf16[2,16,1152]{2,1,0:T(8,128)(2,1)S(1)}, f32[8,256]{1,0:T(8,128)S(1)}, f32[8,256]{1,0:T(8,128)}, bf16[8,16,1152]{2,1,0:T(8,128)(2,...) while((s32[]{:T(128)}, ...), condition=%wide.region_5.6_spmd, body=%wide.region_0.5_spmd.sunk | while | flops 343376224 | bytes 12854366 | solution.py:192
  208.1 5.9 fusion.132
  219.4 2.4 collective-permute-done
  226.8 5.9 fusion.132
  238.1 2.4 collective-permute-done
  245.5 5.9 fusion.132
  264.2 5.9 fusion.132
  282.9 5.9 fusion.132
  301.6 5.9 fusion.132
  320.3 5.9 fusion.132
  339.0 5.9 fusion.132
  357.7 5.9 fusion.132
  376.4 5.9 fusion.132
  387.7 2.4 collective-permute-done
  395.1 5.9 fusion.132
  413.8 5.9 fusion.132
  432.5 5.9 fusion.132
  451.2 5.9 fusion.132
  469.9 5.9 fusion.132
  488.6 5.9 fusion.132
  507.3 5.9 fusion.132
  526.0 5.9 fusion.132
  544.7 5.9 fusion.132
  561.3 6.4 psum.14
  575.7 5.2 fusion.33
  582.0 3.3 fusion.80
  585.3 99.1 %reduce-scatter.3.cloned.1.call-done = f32[144,1152]{1,0:T(8,128)} async-done(((f32[1152,1152]{1,0:T(8,128)}), f32[144,1152]{1,0:T(8,128)}) %reduce-scatter.3.cloned.1.call-update) | async-done | bytes 663568 | tf_op jit(solution)/shard_map/reduce_scatter | solution.py:249
  684.5 108.3 %reduce-scatter.5.cloned.1.call-done = f32[144,1152]{1,0:T(8,128)} async-done(((f32[1152,1152]{1,0:T(8,128)}), f32[144,1152]{1,0:T(8,128)}) %reduce-scatter.5.cloned.1.call-update) | async-done | bytes 663568 | tf_op jit(solution)/shard_map/reduce_scatter | solution.py:250
  (694 shorter events, 235.3 us)
Async XLA Ops:
  8.0 15.0 %copy-start = (bf16[1152,1152]{1,0:T(8,128)(2,1)S(1)}, bf16[1152,1152]{1,0:T(8,128)(2,1)}, u32[]{:S(2)}) copy-start(bf16[1152,1152]{1,0:T(8,128)(2,1)} %param.32) | copy-start | bytes 7962628
  8.0 51.7 %all-reduce.2.cloned.1.call-start = ((), (), s32[]{:S(2)}) async-start(), calls=%async_computation.2 | async-start | bytes 589824 | tf_op jit(solution)/shard_map/psum | solution.py:217
  9.5 7.2 copy-start.14
  17.5 44.5 %copy-start.7 = (f32[8,1152]{1,0:T(8,128)}, f32[8,1152]{1,0:T(8,128)S(1)}, u32[]{:S(2)}) copy-start(f32[8,1152]{1,0:T(8,128)S(1)} %get-tuple-element.419) | copy-start | bytes 110596
  24.4 38.8 %copy-start.8 = (bf16[1152,16]{0,1:T(8,128)(2,1)S(1)}, bf16[1152,16]{0,1:T(8,128)(2,1)}, u32[]{:S(2)}) copy-start(bf16[1152,16]{0,1:T(8,128)(2,1)} %param.26) | copy-start | bytes 110596
  24.4 91.9 %all-gather.5.cloned.1.call-start = ((), (), s32[]{:S(2)}) async-start(), calls=%async_computation.5 | async-start | bytes 5971968 | tf_op jit(solution)/shard_map/all_gather | solution.py:124
  25.0 179.4 %copy-start.9 = (bf16[16,1152]{1,0:T(8,128)(2,1)S(1)}, bf16[16,1152]{1,0:T(8,128)(2,1)}, u32[]{:S(2)}) copy-start(bf16[16,1152]{1,0:T(8,128)(2,1)} %param.25) | copy-start | bytes 110596
  25.0 179.4 %copy-start.15 = (s32[8]{0:T(128)S(1)}, s32[8]{0:T(128)}, u32[]{:S(2)}) copy-start(s32[8]{0:T(128)} %param.21) | copy-start | bytes 100
  25.0 178.0 %all-gather.7.cloned.1.call-start = ((), (), s32[]{:S(2)}) async-start(), calls=%async_computation.6 | async-start | bytes 5971968 | tf_op jit(solution)/shard_map/all_gather | solution.py:125
  25.6 658.9 %reduce-scatter.3.cloned.1.call-start = ((), (), s32[]{:S(2)}) async-start(), calls=%async_computation.3 | async-start | bytes 5971968 | tf_op jit(solution)/shard_map/reduce_scatter | solution.py:249
  217.9 3.8 collective-permute-start
  236.6 3.8 collective-permute-start
  255.3 3.8 collective-permute-start
  274.0 3.8 collective-permute-start
  292.8 3.8 collective-permute-start
  311.5 3.8 collective-permute-start
  330.2 3.8 collective-permute-start
  348.9 3.8 collective-permute-start
  367.6 3.8 collective-permute-start
  386.3 3.8 collective-permute-start
  405.0 3.8 collective-permute-start
  423.7 3.8 collective-permute-start
  442.4 3.8 collective-permute-start
  461.1 3.8 collective-permute-start
  479.8 3.8 collective-permute-start
  498.5 3.8 collective-permute-start
  517.2 3.8 collective-permute-start
  535.9 3.8 collective-permute-start
  554.6 3.8 collective-permute-start
  559.8 14.2 %copy-start.1 = (bf16[8,16,1152]{2,1,0:T(8,128)(2,1)S(1)}, bf16[8,16,1152]{2,1,0:T(8,128)(2,1)}, u32[]{:S(2)}) copy-start(bf16[8,16,1152]{2,1,0:T(8,128)(2,1)} %all-reduce.2.cloned.1.call-done) | copy-start | bytes 884740
  559.8 15.9 %copy-start.5 = (bf16[8,16,1152]{2,1,0:T(8,128)(2,1)S(1)}, bf16[8,16,1152]{2,1,0:T(8,128)(2,1)}, u32[]{:S(2)}) copy-start(bf16[8,16,1152]{2,1,0:T(8,128)(2,1)} %copy-done.4) | copy-start | bytes 884740
  580.9 211.8 %reduce-scatter.5.cloned.1.call-start = ((), (), s32[]{:S(2)}) async-start(), calls=%async_computation.4 | async-start | bytes 5971968 | tf_op jit(solution)/shard_map/reduce_scatter | solution.py:250
  (8 other events, 19.5 us)
Sparse Core Ops, SparseCore 0:
  24.5 35.1 all-reduce.1
Sparse Core Ops, SparseCore 1:
  27.1 89.1 all-gather.4
  118.4 84.7 all-gather.6
  581.0 103.4 reduce-scatter.2
  688.7 104.0 reduce-scatter.4
where the time goes:
time: 807 us; the launch traced here: 800 us
  waiting for transfers between devices  425 us (53%)
  matrix products  131 us (16%)
  other arithmetic  105 us (13%)
  local copies, waits for them, and re-layouts  81.9 us (10%)
  loops' own time  34.9 us (4%)
  between operations  16 us (2%)
    dot_general x19, matrix products, mlp_block(): jnp.dot(hidden, down_proj, preferred_element_type=jnp.float32)  111 us
    reduce_scatter x1, waiting for transfers between devices, body(): lax.psum_scatter(local_down, 'dp', scatter_dimension=0, tiled=True)  108 us
    reduce_scatter x1, waiting for transfers between devices, body(): lax.psum_scatter(local_up, 'dp', scatter_dimension=0, tiled=True)  99.1 us
    all_gather x1, waiting for transfers between devices, body(): lax.all_gather(teacher_down[0], 'dp', axis=0, tiled=True)  86.8 us
    all_gather x1, waiting for transfers between devices, body(): lax.all_gather(teacher_up[0], 'dp', axis=0, tiled=True)  52.2 us
    ppermute x19, waiting for transfers between devices, shifted(): lax.ppermute(shard, axis, [(i, (i + by) % length) for i in range(length)])  45 us
    another operation x1, loops' own time, body(): lax.fori_loop(0, 2 * micro_count + section_count - 1, advance, start_tuple)  34.9 us
    psum x1, waiting for transfers between devices, body(): lax.psum(partial_value.astype(jnp.bfloat16), 'section').astype(jnp.float32)  32.1 us
  transfers between devices with their start and end apart: 24, of which 24 were waited for; matrix products, arithmetic and copies ran while one was open for 4% of the time, Pallas kernels for 0%

commit v1 on v0

v1 whole, which is shorter than its diff:
```python
import math

import jax
import jax.numpy as jnp
from jax import lax
from jax.sharding import PartitionSpec as P

CH = 16
TSTEPS = 1000
STRIDE = 125


norm_eps = 1e-06


def shifted(shard, axis, by):
    length = lax.axis_size(axis)
    return lax.ppermute(shard, axis, [(i, (i + by) % length) for i in range(length)])


def from_root(shard, axis, root):
    mine = lax.axis_index(axis) == root
    return lax.psum(jnp.where(mine, shard, jnp.zeros_like(shard)), axis)


def layer_norm(values):
    center = values - jnp.mean(values, axis=-1, keepdims=True)
    spread = jnp.mean(center * center, axis=-1, keepdims=True)
    return center * lax.rsqrt(spread + norm_eps)


def sinusoid(step_ids, model_width):
    half_width = model_width // 2
    frequency = jnp.exp(-math.log(10000.0) * jnp.arange(half_width, dtype=jnp.float32) / half_width)
    phase_arg = step_ids.astype(jnp.float32)[:, None] * frequency[None, :]
    return jnp.concatenate([jnp.cos(phase_arg), jnp.sin(phase_arg)], axis=-1)


def plan(step_ids):
    angle_t = 0.5 * math.pi / TSTEPS * step_ids.astype(jnp.float32)
    return (jnp.cos(angle_t), jnp.sin(angle_t))


def embed_tokens(latent, embed_in):
    leading = latent.shape[0]
    patches = latent.reshape(leading * (latent.shape[1] // CH), CH).astype(jnp.bfloat16)
    tokens = jnp.dot(patches, embed_in, preferred_element_type=jnp.float32)
    return tokens.reshape(leading, latent.shape[1] // CH, embed_in.shape[1]).astype(jnp.bfloat16)


def mlp_block(inputs, modulation, up_proj, down_proj):
    groups, seq_len, model_width = inputs.shape
    residual_in = inputs.astype(jnp.float32)
    shift_rows = modulation[:, 0, None, :]
    scale_rows = modulation[:, 1, None, :]
    gate_rows = modulation[:, 2, None, :]
    normed = (layer_norm(residual_in) * (1.0 + scale_rows) + shift_rows).astype(jnp.bfloat16)
    pre_act = jnp.dot(
        normed.reshape(groups * seq_len, model_width), up_proj, preferred_element_type=jnp.float32
    )
    hidden = jax.nn.gelu(pre_act, approximate=True).astype(jnp.bfloat16)
    mixed = jnp.dot(hidden, down_proj, preferred_element_type=jnp.float32).reshape(
        groups, seq_len, model_width
    )
    return (residual_in + gate_rows * mixed).astype(jnp.bfloat16)


def velocity(states, embed_out):
    groups, seq_len, model_width = states.shape
    normed = layer_norm(states.astype(jnp.float32)).astype(jnp.bfloat16)
    result = jnp.dot(
        normed.reshape(groups * seq_len, model_width), embed_out, preferred_element_type=jnp.float32
    )
    return result.reshape(groups, seq_len * embed_out.shape[1])


def ddim_step(latent, predicted, time_now, time_next):
    alpha_now, sigma_now = plan(time_now)
    alpha_next, sigma_next = plan(time_next)
    clean_est = alpha_now[:, None] * latent - sigma_now[:, None] * predicted
    noise_est = sigma_now[:, None] * latent + alpha_now[:, None] * predicted
    return alpha_next[:, None] * clean_est + sigma_next[:, None] * noise_est


def gelu_slope(pre_act):
    return jax.vjp(lambda inner: jax.nn.gelu(inner, approximate=True), pre_act)[1](
        jnp.ones_like(pre_act)
    )[0]


def run_chunks(count, one, operands, shared):
    if count == 1:
        return one(operands, *shared)

    def step(carry, piece):
        out = one(piece, *shared)
        return (carry[0] + out[0], carry[1] + out[1]), None

    split = [a.reshape((count, a.shape[0] // count) + a.shape[1:]) for a in operands]
    shapes = jax.eval_shape(one, [a[0] for a in split], *shared)
    zeros = tuple(jnp.zeros(s.shape, s.dtype) for s in shapes)
    return lax.scan(step, zeros, split)[0]


def teacher_chain(first_in, noised, guidance, step_index, mods, up, down, embed_in, embed_out):
    section_count = lax.axis_size("section")
    section_at = lax.axis_index("section")
    micro, seq_len, model_width = first_in.shape

    def paired(tokens):
        return jnp.broadcast_to(tokens[:, None], (micro, 2, seq_len, model_width)).reshape(
            2 * micro, seq_len, model_width
        )

    latent = noised
    states = paired(first_in)
    for which_step in range(2):
        mod = mods[which_step].reshape(2 * micro, 3, model_width)
        if which_step:
            states = paired(embed_tokens(latent, embed_in))
        for layer in range(section_count):
            states = mlp_block(states, mod, up, down)
            if layer < section_count - 1:
                states = lax.ppermute(states, "section", [(layer, layer + 1)])
        predicted = velocity(states, embed_out).reshape(micro, 2, -1)
        weight = guidance[:, None]
        guided = (1.0 + weight) * predicted[:, 0] - weight * predicted[:, 1]
        time_now = step_index - which_step * STRIDE
        stepped = ddim_step(latent, guided, time_now, time_now - STRIDE)
        if which_step == 0:
            returned = lax.ppermute(
                stepped, "section", [(section_count - 1, 0)]
            )
            latent = jnp.where(section_at == section_count - 1, stepped, returned)
    return stepped


def body(
    clean_latent,
    noise_draw,
    step_index,
    labels,
    guide_level,
    class_table,
    embed_in,
    embed_out,
    teacher_up,
    teacher_down,
    teacher_gain,
    teacher_bias,
    student_up,
    student_down,
    student_gain,
    student_bias,
    guide_vec,
):
    section_count = lax.axis_size("section")
    dp_count = lax.axis_size("dp")
    section_at = lax.axis_index("section")
    dp_at = lax.axis_index("dp")
    micro = clean_latent.shape[0]
    width = clean_latent.shape[1]
    seq_len = width // CH
    model_width = class_table.shape[1]
    up = lax.all_gather(teacher_up[0], "dp", axis=0, tiled=True)
    down = lax.all_gather(teacher_down[0], "dp", axis=0, tiled=True)
    alpha_t, sigma_t = plan(step_index)
    noised = alpha_t[:, None] * clean_latent + sigma_t[:, None] * noise_draw
    guidance = 0.5 * guide_level.astype(jnp.float32)
    label_rows = jnp.take(class_table, labels, axis=0).astype(jnp.float32)
    null_row = class_table[class_table.shape[0] - 1].astype(jnp.float32)
    wave_rows = jnp.stack(
        [sinusoid(step_index - step_k * STRIDE, model_width) for step_k in range(2)]
    )
    conditions = jnp.stack(
        [wave_rows + label_rows[None], wave_rows + null_row[None, None, :]], axis=2
    )
    mods = (
        conditions[:, :, :, None, :] * teacher_gain[0][None, None, None]
        + teacher_bias[0][None, None, None]
    )
    first_in = embed_tokens(noised, embed_in)
    ending = teacher_chain(
        first_in, noised, guidance, step_index, mods, up, down, embed_in, embed_out
    )
    alpha_end, sigma_end = plan(step_index - 2 * STRIDE)
    sigma_ratio = sigma_end / sigma_t
    goal_latent = (ending - sigma_ratio[:, None] * noised) / (alpha_end - sigma_ratio * alpha_t)[
        :, None
    ]

    packed = jnp.concatenate(
        [
            noised,
            step_index.astype(jnp.float32)[:, None],
            labels.astype(jnp.float32)[:, None],
            guide_level.astype(jnp.float32)[:, None],
        ],
        axis=1,
    )
    packed = lax.all_gather(packed, "dp", axis=0, tiled=True)
    all_noised = packed[:, :width]
    all_steps = packed[:, width].astype(jnp.int32)
    all_labels = packed[:, width + 1].astype(jnp.int32)
    all_guidance = 0.5 * packed[:, width + 2]

    def student_front(noised, steps, labels, guidance, student_up):
        rows = noised.shape[0] * seq_len
        label_rows = jnp.take(class_table, labels, axis=0).astype(jnp.float32)
        cond = sinusoid(steps, model_width) + label_rows + guidance[:, None] * guide_vec[None, :]
        modulation = cond[:, None, :] * student_gain[None] + student_bias[None]
        residual_in = embed_tokens(noised, embed_in).astype(jnp.float32)
        normed = (
            (layer_norm(residual_in) * (1.0 + modulation[:, 1, None, :]) + modulation[:, 0, None, :])
            .astype(jnp.bfloat16)
            .reshape(rows, model_width)
        )
        pre_act = jnp.dot(normed, student_up, preferred_element_type=jnp.float32)
        hidden = jax.nn.gelu(pre_act, approximate=True).astype(jnp.bfloat16)
        return residual_in, modulation[:, 2, None, :], normed, pre_act, hidden

    own = student_front(noised, step_index, labels, guidance, student_up)
    partial_value = jnp.dot(own[4], student_down, preferred_element_type=jnp.float32)
    mixed = lax.psum(partial_value.astype(jnp.bfloat16), "section")
    all_mixed = lax.all_gather(mixed, "dp", axis=0, tiled=True)
    all_mixed = all_mixed.reshape(micro * dp_count, seq_len, model_width)

    total = micro * dp_count
    element_count = total * width
    up_share = model_width // dp_count
    down_share = student_down.shape[0] // dp_count

    mine = section_at == section_count - 1
    gathered = lax.all_gather(goal_latent, ("section", "dp"), axis=0, tiled=True)
    all_target = gathered[total * (section_count - 1):]
    distill_target = lax.dynamic_slice_in_dim(all_target, dp_at * micro, micro, 0)

    def student_grads(operands, student_up, student_down):
        noised, steps, labels, guidance, mixed, target = operands
        count = noised.shape[0]
        rows = count * seq_len
        residual_in, gate_rows, normed, pre_act, hidden = student_front(
            noised, steps, labels, guidance, student_up
        )
        state_rows = residual_in + gate_rows * mixed.astype(jnp.float32)
        alpha_t, sigma_t = plan(steps)
        normed_out, pullback = jax.vjp(layer_norm, state_rows)
        predicted = jnp.dot(
            normed_out.astype(jnp.bfloat16).reshape(rows, model_width),
            embed_out,
            preferred_element_type=jnp.float32,
        ).reshape(count, width)
        estimate = alpha_t[:, None] * noised - sigma_t[:, None] * predicted
        weight = jnp.maximum(alpha_t * alpha_t / (sigma_t * sigma_t), 1.0)
        slope_pred = -2.0 / element_count * (sigma_t * weight)[:, None] * (estimate - target)
        back_norm = jnp.dot(
            slope_pred.reshape(rows, CH),
            embed_out.astype(jnp.float32).T,
            precision=lax.Precision.HIGHEST,
        )
        back_state = pullback(back_norm.reshape(count, seq_len, model_width))[0]
        back_part = (gate_rows * back_state).astype(jnp.bfloat16).reshape(rows, model_width)
        back_hidden = lax.dot_general(
            back_part, student_down, (((1,), (1,)), ((), ())), preferred_element_type=jnp.float32
        )
        back_pre = (back_hidden * gelu_slope(pre_act)).astype(jnp.bfloat16)
        normed_share = lax.dynamic_slice_in_dim(normed, dp_at * up_share, up_share, 1)
        hidden_share = lax.dynamic_slice_in_dim(hidden, dp_at * down_share, down_share, 1)
        contract_rows = (((0,), (0,)), ((), ()))
        return (
            lax.dot_general(
                normed_share, back_pre, contract_rows, preferred_element_type=jnp.float32
            ),
            lax.dot_general(
                hidden_share, back_part, contract_rows, preferred_element_type=jnp.float32
            ),
        )

    operands = [all_noised, all_steps, all_labels, all_guidance, all_mixed, all_target]
    grad_up, grad_down = run_chunks(
        max(1, dp_count // 8), student_grads, operands, (student_up, student_down)
    )
    return (distill_target, grad_up, grad_down)


def solution(mesh):
    return jax.shard_map(
        body,
        mesh=mesh,
        in_specs=(
            P("dp", None),
            P("dp", None),
            P("dp"),
            P("dp"),
            P("dp"),
            P(),
            P(),
            P(),
            P("section", "dp", None),
            P("section", "dp", None),
            P("section", None, None),
            P("section", None, None),
            P(None, "section"),
            P("section", None),
            P(),
            P(),
            P(),
        ),
        out_specs=(P("dp", None), P("dp", "section"), P(("section", "dp"), None)),
        check_vma=False,
    )
```

time: 807 us -> 507 us (0.63)
  waiting for transfers between devices: 425 us -> 177 us
  blocking collectives: 6.44 us -> 103 us
  local copies, waits for them, and re-layouts: 81.9 us -> 22.7 us
  other arithmetic: 105 us -> 63.7 us
  loops' own time: 34.9 us -> 0 us
  matrix products: 131 us -> 105 us
    reduce_scatter x2 -> x0, waiting for transfers between devices: 207 us -> none  [the longest x1 108 us: body(): lax.psum_scatter(local_down, 'dp', scatter_dimension=0, tiled=True)]
    all_gather x0 -> x2, blocking collectives: none -> 103 us  [the longest x1 70.9 us: body(): lax.all_gather(goal_latent, ('section', 'dp'), axis=0, tiled=True)]
    dot_general x19 -> x8, matrix products: 111 us -> 68.5 us  [mlp_block(): jnp.dot(hidden, down_proj, preferred_element_type=jnp.float32)]
    ppermute x19 -> x7, waiting for transfers between devices: 45 us -> 3.44 us  [the longest x1 3.43 us: teacher_chain(): returned = lax.ppermute(stepped, 'section', [(section_count - 1, 0)])]
    another operation x1 -> x0, loops' own time: 34.9 us -> none  [body(): lax.fori_loop(0, 2 * micro_count + section_count - 1, advance, start_tuple)]
    all_gather x2 -> x3, waiting for transfers between devices: 139 us -> 172 us  [the longest x1 87.1 us: body(): up = lax.all_gather(teacher_up[0], 'dp', axis=0, tiled=True)]
    psum x1, waiting for transfers between devices: 32.1 us -> 0.01 us  [body(): mixed = lax.psum(partial_value.astype(jnp.bfloat16), 'section')]
    dynamic_update_slice x19 -> x0, other arithmetic: 26.3 us -> none  [record(): lax.dynamic_update_index_in_dim(buffer, jnp.where(write_flag, values, cur...]
  transfers between devices with their start and end apart: 24 -> 11, of which waited for: 24 -> 4; matrix products, arithmetic and copies ran while one was open for 4% -> 21% of each run, Pallas kernels for 0% -> 0%
where the time goes in v1:
time: 507 us; the launch traced here: 497 us
  waiting for transfers between devices  177 us (35%)
  matrix products  105 us (21%)
  blocking collectives  103 us (20%)
  other arithmetic  63.7 us (13%)
  local copies, waits for them, and re-layouts  22.7 us (4%)
  between operations  17 us (3%)
  starting transfers between devices  7.81 us (2%)
    all_gather x1, waiting for transfers between devices, body(): up = lax.all_gather(teacher_up[0], 'dp', axis=0, tiled=True)  87.1 us
    all_gather x1, waiting for transfers between devices, body(): down = lax.all_gather(teacher_down[0], 'dp', axis=0, tiled=True)  72.3 us
    all_gather x1, blocking collectives, body(): lax.all_gather(goal_latent, ('section', 'dp'), axis=0, tiled=True)  70.9 us
    dot_general x8, matrix products, mlp_block(): jnp.dot(hidden, down_proj, preferred_element_type=jnp.float32)  68.5 us
    all_gather x1, blocking collectives, body(): packed = lax.all_gather(packed, 'dp', axis=0, tiled=True)  32.5 us
    all_gather x1, waiting for transfers between devices, body(): all_mixed = lax.all_gather(mixed, 'dp', axis=0, tiled=True)  13.2 us
    convert_element_type x6, other arithmetic, mlp_block(): return (residual_in + gate_rows * mixed).astype(jnp.bfloat16)  13 us
    convert_element_type x8, other arithmetic, mlp_block(): (layer_norm(residual_in) * (1.0 + scale_rows) + shift_rows).astype(jnp.bf...  11.1 us
  transfers between devices with their start and end apart: 11, of which 4 were waited for; matrix products, arithmetic and copies ran while one was open for 21% of the time, Pallas kernels for 0%

profile of v1, /device:TPU:0, one launch (start us, length us, event | category | flops | bytes accessed | tf_op | source)
XLA Modules:
  0.0 497.3 jit_solution(11261445627594501748)
XLA Ops:
  10.9 2.5 gather_fusion.1
  28.3 72.3 %all-gather.10.cloned.1.call-done = bf16[1,2304,1152]{2,1,0:T(8,128)(2,1)} async-done(((bf16[1,288,1152]{2,1,0:T(8,128)(2,1)}), bf16[1,2304,1152]{2,1,0:T(8,128)(2,1)}) %all-gather.10.cloned.1.call-update) | async-done | bytes 5308432 | tf_op jit(solution)/shard_map/all_gather | solution.py:166
  100.5 87.1 %all-gather.8.cloned.1.call-done = bf16[1,1152,2304]{2,1,0:T(8,128)(2,1)} async-done(((bf16[1,144,2304]{2,1,0:T(8,128)(2,1)}), bf16[1,1152,2304]{2,1,0:T(8,128)(2,1)}) %all-gather.8.cloned.1.call-update) | async-done | bytes 5308432 | tf_op jit(solution)/shard_map/all_gather | solution.py:165
  187.6 8.6 %fusion.16 = f32[256,1152]{1,0:T(8,128)} fusion(bf16[1,2304,1152]{2,1,0:T(8,128)(2,1)} %all-gather.10.cloned.1.call-done, bf16[256,1152]{1,0:T(8,128)(2,1)} %fusion.199, bf16[1,1152,2304]{2,1,0:T(8,128)(2,1)} %all-gather.8.cloned.1.call-done), kind=kOutput, calls=%fused_computation.24 | convolution fusion | flops 2723217408 | bytes 12386304 | tf_op jit(solution)/shard_map/dot_general | solution.py:62
  196.2 2.2 fusion.201
  199.7 3.7 convolution_convert_fusion.1
  203.8 32.5 %all_gather.18 = f32[64,259]{1,0:T(8,128)} all-gather(f32[8,259]{1,0:T(8,128)S(1)} %pad_maximum_fusion.3), channel_id=1, replica_groups=mesh['section'=4,'dp'=8] {'dp'}, dimensions={0}, use_global_device_ids=true | all-gather | bytes 74592 | tf_op jit(solution)/shard_map/all_gather | solution.py:201
  238.1 8.6 %fusion.14 = f32[256,1152]{1,0:T(8,128)} fusion(bf16[1,2304,1152]{2,1,0:T(8,128)(2,1)} %all-gather.10.cloned.1.call-done, bf16[256,1152]{1,0:T(8,128)(2,1)} %bitcast.279, bf16[1,1152,2304]{2,1,0:T(8,128)(2,1)} %all-gather.8.cloned.1.call-done), kind=kOutput, calls=%fused_computation.22 | convolution fusion | flops 2723217408 | bytes 12386304 | tf_op jit(solution)/shard_map/dot_general | solution.py:62
  246.6 2.2 fusion.190
  251.0 3.4 gather_fusion
  260.7 8.6 %fusion.12 = f32[256,1152]{1,0:T(8,128)} fusion(bf16[1,2304,1152]{2,1,0:T(8,128)(2,1)} %all-gather.10.cloned.1.call-done, bf16[256,1152]{1,0:T(8,128)(2,1)} %bitcast.280, bf16[1,1152,2304]{2,1,0:T(8,128)(2,1)} %all-gather.8.cloned.1.call-done), kind=kOutput, calls=%fused_computation.20 | convolution fusion | flops 2723217408 | bytes 12386304 | tf_op jit(solution)/shard_map/dot_general | solution.py:62
  269.3 2.3 fusion.191
  277.1 8.5 %fusion.10 = f32[256,1152]{1,0:T(8,128)} fusion(bf16[1,2304,1152]{2,1,0:T(8,128)(2,1)} %all-gather.10.cloned.1.call-done, bf16[256,1152]{1,0:T(8,128)(2,1)} %bitcast.278, bf16[1,1152,2304]{2,1,0:T(8,128)(2,1)} %all-gather.8.cloned.1.call-done), kind=kOutput, calls=%fused_computation.18 | convolution fusion | flops 2723217408 | bytes 12386304 | tf_op jit(solution)/shard_map/dot_general | solution.py:62
  289.9 3.4 collective-permute-done.3
  295.9 8.5 %fusion.8 = f32[256,1152]{1,0:T(8,128)} fusion(bf16[1,2304,1152]{2,1,0:T(8,128)(2,1)} %all-gather.10.cloned.1.call-done, bf16[256,1152]{1,0:T(8,128)(2,1)} %fusion.196, bf16[1,1152,2304]{2,1,0:T(8,128)(2,1)} %all-gather.8.cloned.1.call-done), kind=kOutput, calls=%fused_computation.16 | convolution fusion | flops 2723217408 | bytes 12386304 | tf_op jit(solution)/shard_map/dot_general | solution.py:62
  304.4 2.3 fusion.198
  313.6 13.2 %all-gather.6.cloned.1.call-done = bf16[1024,1152]{1,0:T(8,128)(2,1)} async-done(((bf16[128,1152]{1,0:T(8,128)(2,1)}), bf16[1024,1152]{1,0:T(8,128)(2,1)}) %all-gather.6.cloned.1.call-update) | async-done | bytes 2359312 | tf_op jit(solution)/shard_map/all_gather | solution.py:225
  326.8 4.1 fusion.45
  333.2 8.6 %fusion.6 = f32[256,1152]{1,0:T(8,128)} fusion(bf16[1,2304,1152]{2,1,0:T(8,128)(2,1)} %all-gather.10.cloned.1.call-done, bf16[256,1152]{1,0:T(8,128)(2,1)} %bitcast.281, bf16[1,1152,2304]{2,1,0:T(8,128)(2,1)} %all-gather.8.cloned.1.call-done), kind=kOutput, calls=%fused_computation.14 | convolution fusion | flops 2723217408 | bytes 12386304 | tf_op jit(solution)/shard_map/dot_general | solution.py:62
  344.3 2.9 multiply_reduce_fusion.1
  349.5 8.6 %fusion.4 = f32[256,1152]{1,0:T(8,128)} fusion(bf16[1,2304,1152]{2,1,0:T(8,128)(2,1)} %all-gather.10.cloned.1.call-done, bf16[256,1152]{1,0:T(8,128)(2,1)} %bitcast.282, bf16[1,1152,2304]{2,1,0:T(8,128)(2,1)} %all-gather.8.cloned.1.call-done), kind=kOutput, calls=%fused_computation.12 | convolution fusion | flops 2723217408 | bytes 12386304 | tf_op jit(solution)/shard_map/dot_general | solution.py:62
  358.1 2.4 fusion.194
  361.3 2.5 multiply_convert_fusion.1
  367.7 2.1 fusion.165
  369.8 8.6 %fusion.2 = f32[256,1152]{1,0:T(8,128)} fusion(bf16[1,2304,1152]{2,1,0:T(8,128)(2,1)} %all-gather.10.cloned.1.call-done, bf16[256,1152]{1,0:T(8,128)(2,1)} %bitcast.277, bf16[1,1152,2304]{2,1,0:T(8,128)(2,1)} %all-gather.8.cloned.1.call-done), kind=kOutput, calls=%fused_computation.10 | convolution fusion | flops 2723217408 | bytes 12386304 | tf_op jit(solution)/shard_map/dot_general | solution.py:62
  381.3 70.9 %all_gather.17 = f32[256,256]{1,0:T(8,128)S(1)} all-gather(f32[8,256]{1,0:T(8,128)S(1)} %subtract_divide_fusion), channel_id=1, replica_groups=mesh['section'=4,'dp'=8] {'section','dp'}, dimensions={0}, use_global_device_ids=true | all-gather | bytes 270336 | tf_op jit(solution)/shard_map/all_gather | solution.py:234
  454.9 5.5 %multiply_reduce_fusion = (f32[64,16]{1,0:T(8,128)S(1)}, f32[64,16]{1,0:T(8,128)S(1)}, f32[64,16,1152]{2,1,0:T(8,128)S(1)}) fusion(f32[64,16]{1,0:T(8,128)S(1)} %copy-done.16, bf16[64,16,1152]{2,1,0:T(8,128)(2,1)} %bitcast.260, f32[64,1152]{1,0:T(8,128)S(1)} %get-tuple-element.23, bf16[64,16,1152]{2,1,0:T(8,128)(2,1)} %get-tuple-element.72, ...), kind=kOutput, calls=%fused_computation.55 | convolution fusion | flops 235927552 | bytes 9846784 | tf_op jit(solution)/shard_map/dot_general | solution.py:256
  460.5 2.7 fusion.230
  463.3 4.2 multiply_convert_fusion
  467.5 6.1 %add_multiply_fusion = (f32[1024,1152]{1,0:T(8,128)}, f32[1024,1152]{1,0:T(8,128)}) fusion(bf16[1024,1152]{1,0:T(8,128)(2,1)S(1)} %bitcast.267, bf16[1152,1152]{1,0:T(8,128)(2,1)S(1)} %copy-done), kind=kOutput, calls=%fused_computation.58 | convolution fusion | flops 2726166528 | bytes 14450688 | tf_op jit(solution)/shard_map/dot_general | solution.py:218
  473.5 10.2 %fusion.145 = f32[144,1152]{1,0:T(8,128)} fusion(f32[1024,1152]{1,0:T(8,128)} %get-tuple-element.77, bf16[1024,1152]{1,0:T(8,128)(2,1)} %bitcast.263, bf16[1152,1152]{1,0:T(8,128)(2,1)} %param.32, bf16[1024,1152]{1,0:T(8,128)(2,1)} %bitcast.268, s32[]{:T(128)S(6)} %select_n.42), kind=kOutput, calls=%fused_computation.162 | convolution fusion | flops 3080060928 | bytes 10919940 | tf_op jit(solution)/shard_map/dot_general | solution.py:271
  483.7 4.7 fusion.227
  (285 shorter events, 66.6 us)
Async XLA Ops:
  8.0 191.7 %copy-start = (bf16[1152,1152]{1,0:T(8,128)(2,1)S(1)}, bf16[1152,1152]{1,0:T(8,128)(2,1)}, u32[]{:S(2)}) copy-start(bf16[1152,1152]{1,0:T(8,128)(2,1)} %param.31) | copy-start | bytes 7962628
  8.0 12.5 %copy-start.66 = (s32[8]{0:T(128)S(1)}, s32[8]{0:T(128)}, u32[]{:S(2)}) copy-start(s32[8]{0:T(128)} %param.21) | copy-start | bytes 100
  8.0 10.7 %copy-start.42 = (f32[1,3,1152]{2,0,1:T(1,128)S(1)}, f32[1,3,1152]{2,0,1:T(1,128)}, u32[]{:S(2)}) copy-start(f32[1,3,1152]{2,0,1:T(1,128)} %param.29) | copy-start | bytes 41476
  8.0 10.7 %copy-start.41 = (f32[1,3,1152]{2,0,1:T(1,128)S(1)}, f32[1,3,1152]{2,0,1:T(1,128)}, u32[]{:S(2)}) copy-start(f32[1,3,1152]{2,0,1:T(1,128)} %param.30) | copy-start | bytes 41476
  8.0 13.1 %copy-start.44 = (f32[8,256]{1,0:T(8,128)S(1)}, f32[8,256]{1,0:T(8,128)}, u32[]{:S(2)}) copy-start(f32[8,256]{1,0:T(8,128)} %param.19) | copy-start | bytes 24580
  8.1 13.1 %copy-start.43 = (f32[8,256]{1,0:T(8,128)S(1)}, f32[8,256]{1,0:T(8,128)}, u32[]{:S(2)}) copy-start(f32[8,256]{1,0:T(8,128)} %param.20) | copy-start | bytes 24580
  8.1 13.7 %copy-start.30 = (bf16[16,1152]{1,0:T(8,128)(2,1)S(1)}, bf16[16,1152]{1,0:T(8,128)(2,1)}, u32[]{:S(2)}) copy-start(bf16[16,1152]{1,0:T(8,128)(2,1)} %param.25) | copy-start | bytes 110596
  8.1 92.4 %all-gather.10.cloned.1.call-start = ((), (), s32[]{:S(2)}) async-start(), calls=%async_computation.3 | async-start | bytes 5971968 | tf_op jit(solution)/shard_map/all_gather | solution.py:166
  8.8 178.8 %all-gather.8.cloned.1.call-start = ((), (), s32[]{:S(2)}) async-start(), calls=%async_computation.2 | async-start | bytes 5971968 | tf_op jit(solution)/shard_map/all_gather | solution.py:165
  9.6 265.8 %all-reduce.2.cloned.1.call-start = ((), (), s32[]{:S(2)}) async-start(), calls=%async_computation | async-start | bytes 589824 | tf_op jit(solution)/shard_map/psum | solution.py:224
  198.4 38.0 %collective-permute-start = (bf16[16,16,1152]{2,1,0:T(8,128)(2,1)}, bf16[16,16,1152]{2,1,0:T(8,128)(2,1)S(1)}, u32[]{:S(2)}, u32[]{:S(2)}) collective-permute-start(bf16[16,16,1152]{2,1,0:T(8,128)(2,1)} %fusion.201), channel_id=1, source_target_pairs={{0,8},{1,9},{2,10},{3,11},{4,12},{5,13},{6,14},{7,15}} | collective-permute-start | bytes 1769480 | tf_op jit(solution)/shard_map/ppermute | solution.py:124
  203.4 123.4 %all-gather.6.cloned.1.call-start = ((), (), s32[]{:S(2)}) async-start(), calls=%async_computation.1 | async-start | bytes 2654208 | tf_op jit(solution)/shard_map/all_gather | solution.py:225
  248.8 10.2 %collective-permute-start.1 = (bf16[16,16,1152]{2,1,0:T(8,128)(2,1)}, bf16[16,16,1152]{2,1,0:T(8,128)(2,1)S(1)}, u32[]{:S(2)}, u32[]{:S(2)}) collective-permute-start(bf16[16,16,1152]{2,1,0:T(8,128)(2,1)} %fusion.190), channel_id=1, source_target_pairs={{8,16},{9,17},{10,18},{11,19},{12,20},{13,21},{14,22},{15,23}} | collective-permute-start | bytes 1769480 | tf_op jit(solution)/shard_map/ppermute | solution.py:124
  271.6 3.7 collective-permute-start.2
  288.4 5.0 collective-permute-start.3
  289.9 14.5 %copy-start.8 = (f32[16,1152]{1,0:T(8,128)}, f32[16,1152]{1,0:T(8,128)S(1)}, u32[]{:S(2)}) copy-start(f32[16,1152]{1,0:T(8,128)S(1)} %get-tuple-element.31) | copy-start | bytes 221188
  289.9 14.5 %copy-start.11 = (f32[16,1152]{1,0:T(8,128)}, f32[16,1152]{1,0:T(8,128)S(1)}, u32[]{:S(2)}) copy-start(f32[16,1152]{1,0:T(8,128)S(1)} %get-tuple-element.32) | copy-start | bytes 221188
  289.9 14.5 %copy-start.7 = (f32[16,1152]{1,0:T(8,128)}, f32[16,1152]{1,0:T(8,128)S(1)}, u32[]{:S(2)}) copy-start(f32[16,1152]{1,0:T(8,128)S(1)} %get-tuple-element.30) | copy-start | bytes 221188
  306.7 24.8 %collective-permute-start.4 = (bf16[16,16,1152]{2,1,0:T(8,128)(2,1)}, bf16[16,16,1152]{2,1,0:T(8,128)(2,1)S(1)}, u32[]{:S(2)}, u32[]{:S(2)}) collective-permute-start(bf16[16,16,1152]{2,1,0:T(8,128)(2,1)} %fusion.198), channel_id=1, source_target_pairs={{0,8},{1,9},{2,10},{3,11},{4,12},{5,13},{6,14},{7,15}} | collective-permute-start | bytes 1769480 | tf_op jit(solution)/shard_map/ppermute | solution.py:124
  343.3 4.5 collective-permute-start.5
  360.5 6.8 %collective-permute-start.6 = (bf16[16,16,1152]{2,1,0:T(8,128)(2,1)}, bf16[16,16,1152]{2,1,0:T(8,128)(2,1)S(1)}, u32[]{:S(2)}, u32[]{:S(2)}) collective-permute-start(bf16[16,16,1152]{2,1,0:T(8,128)(2,1)} %fusion.194), channel_id=1, source_target_pairs={{16,24},{17,25},{18,26},{19,27},{20,28},{21,29},{22,30},{23,31}} | collective-permute-start | bytes 1769480 | tf_op jit(solution)/shard_map/ppermute | solution.py:124
  380.0 72.2 %copy-start.19 = (f32[64,259]{1,0:T(8,128)S(1)}, f32[64,259]{1,0:T(8,128)}, u32[]{:S(2)}) copy-start(f32[64,259]{1,0:T(8,128)} %all_gather.18) | copy-start | bytes 198916
  380.0 72.2 %copy-start.33 = (f32[64,256]{1,0:T(8,128)S(1)}, f32[64,256]{1,0:T(8,128)}, u32[]{:S(2)}) copy-start(f32[64,256]{1,0:T(8,128)} %reshape.516) | copy-start | bytes 196612
  380.0 72.2 %copy-start.57 = (f32[64]{0:T(128)S(1)}, f32[64]{0:T(128)}, u32[]{:S(2)}) copy-start(f32[64]{0:T(128)} %get-tuple-element.8) | copy-start | bytes 772
  380.0 72.2 %copy-start.58 = (f32[64]{0:T(128)S(1)}, f32[64]{0:T(128)}, u32[]{:S(2)}) copy-start(f32[64]{0:T(128)} %get-tuple-element.9) | copy-start | bytes 772
  380.1 72.2 %copy-start.59 = (f32[64]{0:T(128)S(1)}, f32[64]{0:T(128)}, u32[]{:S(2)}) copy-start(f32[64]{0:T(128)} %get-tuple-element.10) | copy-start | bytes 772
  380.1 74.7 %copy-start.16 = (f32[64,16]{1,0:T(8,128)S(1)}, f32[64,16]{1,0:T(8,128)}, u32[]{:S(2)}) copy-start(f32[64,16]{1,0:T(8,128)} %broadcast_multiply_fusion) | copy-start | bytes 12292
  380.1 74.7 %copy-start.26 = (bf16[1152,16]{0,1:T(8,128)(2,1)S(1)}, bf16[1152,16]{0,1:T(8,128)(2,1)}, u32[]{:S(2)}) copy-start(bf16[1152,16]{0,1:T(8,128)(2,1)} %param.26) | copy-start | bytes 110596
  454.8 5.6 %copy-start.3 = (bf16[64,16,1152]{2,1,0:T(8,128)(2,1)S(1)}, bf16[64,16,1152]{2,1,0:T(8,128)(2,1)}, u32[]{:S(2)}) copy-start(bf16[64,16,1152]{2,1,0:T(8,128)(2,1)} %get-tuple-element.72) | copy-start | bytes 7077892
  454.8 5.6 %copy-start.4 = (bf16[1024,1152]{1,0:T(8,128)(2,1)S(1)}, bf16[1024,1152]{1,0:T(8,128)(2,1)}, u32[]{:S(2)}) copy-start(bf16[1024,1152]{1,0:T(8,128)(2,1)} %all-gather.6.cloned.1.call-done) | copy-start | bytes 7077892
  454.9 5.6 %copy-start.29 = (f32[64,16]{1,0:T(8,128)S(1)}, f32[64,16]{1,0:T(8,128)}, u32[]{:S(2)}) copy-start(f32[64,16]{1,0:T(8,128)} %fusion.254) | copy-start | bytes 12292
  467.5 6.1 %copy-start.6 = (bf16[64,16,1152]{2,1,0:T(8,128)(2,1)}, bf16[64,16,1152]{2,1,0:T(8,128)(2,1)S(1)}, u32[]{:S(2)}) copy-start(bf16[64,16,1152]{2,1,0:T(8,128)(2,1)S(1)} %get-tuple-element.22) | copy-start | bytes 7077892
  (49 other events, 134.4 us)
Sparse Core Ops, SparseCore 0:
  11.1 89.4 all-gather.9
  102.7 84.8 all-gather.7
  275.5 51.2 all-gather.5
Sparse Core Ops, SparseCore 1:
  203.5 29.9 all-reduce.1

commit v2 on v1

--- a/solution.py
+++ b/solution.py
@@ -1,8 +1,11 @@
+import functools
 import math
 
 import jax
 import jax.numpy as jnp
 from jax import lax
+from jax.experimental import pallas as pl
+from jax.experimental.pallas import tpu as pltpu
 from jax.sharding import PartitionSpec as P
 
 CH = 16
@@ -133,6 +136,280 @@
             )
             latent = jnp.where(section_at == section_count - 1, stepped, returned)
     return stepped
+
+
+def chunked_mlp(normed, up_ref, down_ref, width):
+    def piece(j, total):
+        at = pl.ds(pl.multiple_of(j * width, width), width)
+        hidden = jax.nn.gelu(
+            jnp.dot(normed, up_ref[:, at], preferred_element_type=jnp.float32), approximate=True
+        ).astype(jnp.bfloat16)
+        return total + jnp.dot(hidden, down_ref[at, :], preferred_element_type=jnp.float32)
+
+    zero = jnp.zeros((normed.shape[0], down_ref.shape[1]), jnp.float32)
+    return lax.fori_loop(0, up_ref.shape[1] // width, piece, zero)
+
+
+def teacher_kernel(
+    dims,
+    up_shard, down_shard, packed_in, normed_own, stud_up, stud_down,
+    mods, first_in, latent_in, coef, embed_in, embed_out,
+    packed_all, mixed_all, target_all,
+    up, down, parts, states, outs, velo, z_sem_buf, z_in,
+    send, recv,
+):
+    section_count, dp_count, micro, seq_len = dims
+    sec = lax.axis_index("section")
+    me = lax.axis_index("dp")
+    planes = dp_count // 2
+    z, y = me // 2, me % 2
+    z_up = lax.rem(z + 1, planes)
+    z_dn = lax.rem(z + planes - 1, planes)
+    z_op = lax.rem(z + 2, planes)
+    tail = section_count - 1
+
+    def at(zz, yy):
+        return zz * 2 + yy
+
+    peer, above, below = at(z, 1 - y), at(z_up, y), at(z_dn, y)
+    barrier = pltpu.get_barrier_semaphore()
+    for k in range(1, dp_count):
+        pl.semaphore_signal(
+            barrier, inc=1, device_id={"dp": lax.rem(me + k, dp_count)},
+            device_id_type=pl.DeviceIdType.MESH,
+        )
+    for k in range(1, section_count):
+        pl.semaphore_signal(
+            barrier, inc=1, device_id={"section": lax.rem(sec + k, section_count)},
+            device_id_type=pl.DeviceIdType.MESH,
+        )
+    pl.semaphore_wait(barrier, dp_count + section_count - 2)
+
+    count = [0]
+
+    def copy(src, dst, **device):
+        i = count[0]
+        count[0] += 1
+        return pltpu.make_async_remote_copy(
+            src_ref=src, dst_ref=dst, send_sem=send.at[i], recv_sem=recv.at[i],
+            device_id=device, device_id_type=pl.DeviceIdType.MESH,
+        )
+
+    ur, dr = up_shard.shape[0], down_shard.shape[0]
+    ua = (ur // 32) * 16 + 16 * ((ur // 16) % 2)
+    da = (dr // 32) * 16
+
+    def rows(ref, size, who, lo=0, n=None):
+        n = size if n is None else n
+        return ref.at[pl.ds(pl.multiple_of(who * size + lo, 16), n)]
+
+    u, w = functools.partial(rows, up, ur), functools.partial(rows, down, dr)
+
+    def go(c):
+        c.start()
+        return c
+
+    sent = []
+
+    def ship(src, dst, **device):
+        c = go(copy(src, dst, **device))
+        sent.append(c)
+        return c
+
+    own_slot_rows = micro * seq_len
+    packs = []
+    for k in range(1, dp_count):
+        packs.append(
+            ship(packed_in, packed_all.at[me], dp=lax.rem(me + k, dp_count))
+        )
+    u_up = ship(up_shard, u(me), dp=above)
+    u_dn = ship(up_shard, u(me), dp=below)
+    w_y = ship(down_shard, w(me), dp=peer)
+    w_up = ship(down_shard, w(me), dp=above)
+    w_dn = ship(down_shard, w(me), dp=below)
+    u_y = ship(up_shard, u(me), dp=peer)
+    packed_all[me] = packed_in[...]
+    up[pl.ds(pl.multiple_of(me * ur, 16), ur)] = up_shard[...]
+    down[pl.ds(pl.multiple_of(me * dr, 16), dr)] = down_shard[...]
+
+    parts[sec] = chunked_mlp(normed_own[...], stud_up, stud_down, 384).astype(jnp.bfloat16)
+    part_copies = [
+        ship(parts.at[sec], parts.at[sec], section=lax.rem(sec + k, section_count))
+        for k in range(1, section_count)
+    ]
+
+    u_up.wait_recv()
+    f_uu = ship(u(below, 0, ua), u(below, 0, ua), dp=above)
+    f_uy1 = ship(u(below), u(below), dp=peer)
+    u_dn.wait_recv()
+    f_ud = ship(u(above, ua, ur - ua), u(above, ua, ur - ua), dp=below)
+    f_uy2 = ship(u(above), u(above), dp=peer)
+    w_y.wait_recv()
+    v_up = ship(w(peer), w(peer), dp=above)
+    v_dn = ship(w(peer), w(peer), dp=below)
+    w_up.wait_recv()
+    f_wu = ship(w(below, 0, da), w(below, 0, da), dp=above)
+    w_dn.wait_recv()
+    f_wd = ship(w(above, da, dr - da), w(above, da, dr - da), dp=below)
+    f_uu.wait_recv()
+    f_ud.wait_recv()
+    opp = at(z_op, y)
+    f_uy3 = ship(u(opp), u(opp), dp=peer)
+    v_up.wait_recv()
+    pb = at(z_dn, 1 - y)
+    g_wu = ship(w(pb, 0, da), w(pb, 0, da), dp=above)
+    v_dn.wait_recv()
+    pa = at(z_up, 1 - y)
+    g_wd = ship(w(pa, da, dr - da), w(pa, da, dr - da), dp=below)
+
+    for c in part_copies:
+        c.wait_recv()
+    total = parts[0].astype(jnp.float32)
+    for k in range(1, section_count):
+        total = total + parts[k].astype(jnp.float32)
+    mixed_all[me] = total.astype(jnp.bfloat16)
+    for c in (u_y, f_wu, f_wd, f_uy1, f_uy2, f_uy3, g_wu, g_wd):
+        c.wait_recv()
+    mix_copies = [
+        ship(mixed_all.at[me], mixed_all.at[me], dp=lax.rem(me + k, dp_count))
+        for k in range(1, dp_count)
+    ]
+
+    width = first_in.shape[1]
+    nxt = lax.rem(sec + 1, section_count)
+    moves = [copy(outs.at[i], states.at[i], section=nxt) for i in range(4)]
+    z_move = copy(z_sem_buf, z_in, section=0)
+    goal_copies = [
+        copy(target_all.at[me], target_all.at[me], dp=lax.rem(me + k, dp_count))
+        for k in range(1, dp_count)
+    ]
+    final_copies = [
+        copy(target_all, target_all, section=k) for k in range(tail)
+    ]
+
+    for step in range(2):
+        if step == 1:
+            @pl.when(sec == 0)
+            def _():
+                z_move.wait_recv()
+
+        for half in range(2):
+            slot = 2 * step + half
+
+            @pl.when(sec == 0)
+            def _():
+                if step == 0:
+                    states[slot] = first_in[...]
+                else:
+                    states[slot] = lax.dot_general(
+                        z_in[...].astype(jnp.bfloat16), embed_in[...], (((0,), (0,)), ((), ())),
+                        preferred_element_type=jnp.float32,
+                    ).astype(jnp.bfloat16)
+
+            @pl.when(sec > 0)
+            def _():
+                moves[slot].wait_recv()
+
+            residual = states[slot].astype(jnp.float32)
+            shift = mods[step, half, 0][:, None, :]
+            scale = mods[step, half, 1][:, None, :]
+            gate = mods[step, half, 2][:, None, :]
+            cube = layer_norm(residual).reshape(micro, seq_len, width)
+            normed = (cube * (1.0 + scale) + shift).astype(jnp.bfloat16)
+            mixed = chunked_mlp(normed.reshape(micro * seq_len, width), up, down, 768)
+            out = residual.reshape(micro, seq_len, width) + gate * mixed.reshape(
+                micro, seq_len, width
+            )
+            outs[slot] = out.reshape(micro * seq_len, width).astype(jnp.bfloat16)
+
+            @pl.when(sec < tail)
+            def _():
+                moves[slot].start()
+
+            @pl.when(sec == tail)
+            def _():
+                last = layer_norm(outs[slot].astype(jnp.float32)).astype(jnp.bfloat16)
+                velo[half] = lax.dot_general(
+                    embed_out[...], last, (((0,), (1,)), ((), ())),
+                    preferred_element_type=jnp.float32,
+                )
+
+        @pl.when(sec == tail)
+        def _():
+            level = coef[4:5, :]
+            guided = (1.0 + level) * velo[0] - level * velo[1]
+            before = latent_in[...] if step == 0 else z_sem_buf[...]
+            after = coef[2 * step : 2 * step + 1, :] * before + coef[
+                2 * step + 1 : 2 * step + 2, :
+            ] * guided
+            if step == 0:
+                z_sem_buf[...] = after
+                z_move.start()
+                z_move.wait_send()
+            else:
+                target_all[me] = coef[5:6, :] * after + coef[6:7, :] * latent_in[...]
+
+    @pl.when(sec == tail)
+    def _():
+        for c in goal_copies:
+            c.start()
+        for c in goal_copies:
+            c.wait()
+        for c in final_copies:
+            c.start()
+        for c in final_copies:
+            c.wait_send()
+
+    for k in range(tail):
+        @pl.when(sec == k)
+        def _():
+            final_copies[k].wait_recv()
+
+    @pl.when(sec < tail)
+    def _():
+        for c in moves:
+            c.wait_send()
+
+    for c in packs + mix_copies:
+        c.wait_recv()
+    for c in sent:
+        c.wait_send()
+
+
+def teacher_call(dims, operands):
+    section_count, dp_count, micro, seq_len = dims
+    up_shard, down_shard = operands[0], operands[1]
+    width = up_shard.shape[1]
+    model_width = down_shard.shape[1]
+    row_count = micro * seq_len
+    copies = 3 * (dp_count - 1) + 2 * section_count + 64
+    block = (row_count, model_width)
+    vmem = pl.BlockSpec(memory_space=pltpu.VMEM)
+    return pl.pallas_call(
+        functools.partial(teacher_kernel, dims),
+        out_shape=(
+            jax.ShapeDtypeStruct((dp_count,) + operands[2].shape, jnp.float32),
+            jax.ShapeDtypeStruct((dp_count,) + block, jnp.bfloat16),
+            jax.ShapeDtypeStruct((dp_count, CH, row_count), jnp.float32),
+        ),
+        in_specs=[vmem] * len(operands),
+        out_specs=(vmem,) * 3,
+        scratch_shapes=[
+            pltpu.VMEM((up_shard.shape[0] * dp_count, width), jnp.bfloat16),
+            pltpu.VMEM((down_shard.shape[0] * dp_count, model_width), jnp.bfloat16),
+            pltpu.VMEM((section_count,) + block, jnp.bfloat16),
+            pltpu.VMEM((4,) + block, jnp.bfloat16),
+            pltpu.VMEM((4,) + block, jnp.bfloat16),
+            pltpu.VMEM((2, CH, row_count), jnp.float32),
+            pltpu.VMEM((CH, row_count), jnp.float32),
+            pltpu.VMEM((CH, row_count), jnp.float32),
+            pltpu.SemaphoreType.DMA((copies,)),
+            pltpu.SemaphoreType.DMA((copies,)),
+        ],
+        compiler_params=pltpu.CompilerParams(
+            collective_id=0, has_side_effects=True, vmem_limit_bytes=56 << 20
+        ),
+    )(*operands)
 
 
 def body(
@@ -162,8 +439,12 @@
     width = clean_latent.shape[1]
     seq_len = width // CH
     model_width = class_table.shape[1]
-    up = lax.all_gather(teacher_up[0], "dp", axis=0, tiled=True)
-    down = lax.all_gather(teacher_down[0], "dp", axis=0, tiled=True)
+    fused = (
+        dp_count == 8
+        and section_count == 4
+        and teacher_up.shape[1] % 16 == 0
+        and teacher_down.shape[1] % 32 == 0
+    )
     alpha_t, sigma_t = plan(step_index)
     noised = alpha_t[:, None] * clean_latent + sigma_t[:, None] * noise_draw
     guidance = 0.5 * guide_level.astype(jnp.float32)
@@ -180,15 +461,8 @@
         + teacher_bias[0][None, None, None]
     )
     first_in = embed_tokens(noised, embed_in)
-    ending = teacher_chain(
-        first_in, noised, guidance, step_index, mods, up, down, embed_in, embed_out
-    )
     alpha_end, sigma_end = plan(step_index - 2 * STRIDE)
     sigma_ratio = sigma_end / sigma_t
-    goal_latent = (ending - sigma_ratio[:, None] * noised) / (alpha_end - sigma_ratio * alpha_t)[
-        :, None
-    ]
-
     packed = jnp.concatenate(
         [
             noised,
@@ -198,13 +472,7 @@
         ],
         axis=1,
     )
-    packed = lax.all_gather(packed, "dp", axis=0, tiled=True)
-    all_noised = packed[:, :width]
-    all_steps = packed[:, width].astype(jnp.int32)
-    all_labels = packed[:, width + 1].astype(jnp.int32)
-    all_guidance = 0.5 * packed[:, width + 2]
-
-    def student_front(noised, steps, labels, guidance, student_up):
+    def student_normed(noised, steps, labels, guidance):
         rows = noised.shape[0] * seq_len
         label_rows = jnp.take(class_table, labels, axis=0).astype(jnp.float32)
         cond = sinusoid(steps, model_width) + label_rows + guidance[:, None] * guide_vec[None, :]
@@ -215,24 +483,69 @@
             .astype(jnp.bfloat16)
             .reshape(rows, model_width)
         )
+        return residual_in, modulation[:, 2, None, :], normed
+
+    def student_front(noised, steps, labels, guidance, student_up):
+        residual_in, gate_rows, normed = student_normed(noised, steps, labels, guidance)
         pre_act = jnp.dot(normed, student_up, preferred_element_type=jnp.float32)
         hidden = jax.nn.gelu(pre_act, approximate=True).astype(jnp.bfloat16)
-        return residual_in, modulation[:, 2, None, :], normed, pre_act, hidden
-
-    own = student_front(noised, step_index, labels, guidance, student_up)
-    partial_value = jnp.dot(own[4], student_down, preferred_element_type=jnp.float32)
-    mixed = lax.psum(partial_value.astype(jnp.bfloat16), "section")
-    all_mixed = lax.all_gather(mixed, "dp", axis=0, tiled=True)
-    all_mixed = all_mixed.reshape(micro * dp_count, seq_len, model_width)
+        return residual_in, gate_rows, normed, pre_act, hidden
 
     total = micro * dp_count
     element_count = total * width
     up_share = model_width // dp_count
     down_share = student_down.shape[0] // dp_count
 
-    mine = section_at == section_count - 1
-    gathered = lax.all_gather(goal_latent, ("section", "dp"), axis=0, tiled=True)
-    all_target = gathered[total * (section_count - 1):]
+    goal_scale = 1.0 / (alpha_end - sigma_ratio * alpha_t)
+    if fused:
+        own_normed = student_normed(noised, step_index, labels, guidance)[2]
+        pack_pad = -packed.shape[1] % 128
+        packed = jnp.pad(packed, ((0, 0), (0, pack_pad)))
+        coefs = []
+        for step_k in range(2):
+            alpha_k, sigma_k = plan(step_index - step_k * STRIDE)
+            alpha_n, sigma_n = plan(step_index - (step_k + 1) * STRIDE)
+            coefs += [alpha_n * alpha_k + sigma_n * sigma_k, sigma_n * alpha_k - alpha_n * sigma_k]
+        coefs += [guidance, goal_scale, -sigma_ratio * goal_scale, guidance]
+        coefs = jnp.repeat(jnp.stack(coefs), seq_len, axis=1)
+        packed, all_mixed, all_target = teacher_call(
+            (section_count, dp_count, micro, seq_len),
+            (
+                teacher_up[0],
+                teacher_down[0],
+                packed,
+                own_normed,
+                student_up,
+                student_down,
+                mods.transpose(0, 2, 3, 1, 4),
+                first_in.reshape(micro * seq_len, model_width),
+                noised.reshape(micro * seq_len, CH).T,
+                coefs,
+                embed_in,
+                embed_out,
+            ),
+        )
+        packed = packed.reshape(total, packed.shape[-1])
+        all_target = all_target.transpose(0, 2, 1).reshape(total, width)
+    else:
+        up = lax.all_gather(teacher_up[0], "dp", axis=0, tiled=True)
+        down = lax.all_gather(teacher_down[0], "dp", axis=0, tiled=True)
+        ending = teacher_chain(
+            first_in, noised, guidance, step_index, mods, up, down, embed_in, embed_out
+        )
+        goal_latent = (ending - sigma_ratio[:, None] * noised) * goal_scale[:, None]
+        packed = lax.all_gather(packed, "dp", axis=0, tiled=True)
+        own = student_front(noised, step_index, labels, guidance, student_up)
+        partial_value = jnp.dot(own[4], student_down, preferred_element_type=jnp.float32)
+        mixed = lax.psum(partial_value.astype(jnp.bfloat16), "section")
+        all_mixed = lax.all_gather(mixed, "dp", axis=0, tiled=True)
+        gathered = lax.all_gather(goal_latent, ("section", "dp"), axis=0, tiled=True)
+        all_target = gathered[total * (section_count - 1):]
+    all_mixed = all_mixed.reshape(total, seq_len, model_width)
+    all_noised = packed[:, :width]
+    all_steps = packed[:, width].astype(jnp.int32)
+    all_labels = packed[:, width + 1].astype(jnp.int32)
+    all_guidance = 0.5 * packed[:, width + 2]
     distill_target = lax.dynamic_slice_in_dim(all_target, dp_at * micro, micro, 0)
 
     def student_grads(operands, student_up, student_down):

time: 507 us -> 275 us (0.54); the launches traced: 497 us -> 274 us
  Pallas kernels: 0 us -> 204 us
  waiting for transfers between devices: 177 us -> 0 us
  blocking collectives: 103 us -> 0 us
  matrix products: 105 us -> 28.9 us
  other arithmetic: 63.7 us -> 26.5 us
  between operations: 17 us -> 1.03 us
  local copies, waits for them, and re-layouts: 22.7 us -> 13.5 us
  starting transfers between devices: 7.81 us -> 0 us
    pallas_call x0 -> x1, Pallas kernels: none -> 204 us  [teacher_call(): pl.pallas_call(functools.partial(teacher_kernel, dims), out_shape=(jax.Sh...]
    all_gather x3 -> x0, waiting for transfers between devices: 172 us -> none  [the longest x1 87.1 us: body(): up = lax.all_gather(teacher_up[0], 'dp', axis=0, tiled=True)]
    all_gather x2 -> x0, blocking collectives: 103 us -> none  [the longest x1 70.9 us: body(): lax.all_gather(goal_latent, ('section', 'dp'), axis=0, tiled=True)]
    dot_general x11 -> x0, matrix products: 72.7 us -> none  [the longest x8 68.5 us: mlp_block(): jnp.dot(hidden, down_proj, preferred_element_type=jnp.float32)]
    convert_element_type x18 -> x3, other arithmetic: 25.7 us -> 1.8 us  [the longest x1 0.99 us: student_normed(): normed = (layer_norm(residual_in) * (1.0 + modulation[:, 1, None, :]) + m...]
    ppermute x7 -> x0, starting transfers between devices: 7.65 us -> none  [the longest x6 6.19 us: teacher_chain(): states = lax.ppermute(states, 'section', [(layer, layer + 1)])]
  transfers between devices with their start and end apart: 11 -> 0, of which waited for: 4 -> 0; matrix products, arithmetic and copies ran while one was open for 21% -> 0% of each run, Pallas kernels for 0% -> 0%
where the time goes in v2:
time: 275 us; the launch traced here: 274 us
  Pallas kernels  204 us (74%)
  matrix products  28.9 us (11%)
  other arithmetic  26.5 us (10%)
  local copies, waits for them, and re-layouts  13.5 us (5%)
    pallas_call x1, Pallas kernels, teacher_call(): pl.pallas_call(functools.partial(teacher_kernel, dims), out_shape=(jax.Sh...  204 us
    dot_general x1, matrix products, student_grads(): lax.dot_general(normed_share, back_pre, contract_rows, preferred_element_...  9.48 us
    dot_general x1, matrix products, student_front(): pre_act = jnp.dot(normed, student_up, preferred_element_type=jnp.float32)  6.01 us

profile of v2, /device:TPU:0, one launch (start us, length us, event | category | flops | bytes accessed | tf_op | source)
XLA Modules:
  0.0 273.9 jit_solution(4359214399764698137)
XLA Ops:
  3.7 0.8 multiply_bitcast_fusion
  4.5 0.7 convert_reduce_fusion.2
  5.3 0.8 fusion.59
  6.7 2.5 gather_fusion.1
  10.2 0.7 copy_bitcast_fusion
  12.0 0.8 fusion.43
  12.8 0.8 multiply_add_fusion.2
  13.6 0.8 multiply_add_fusion.1.mods
  14.4 1.0 convert_reduce_fusion.1
  15.7 1.0 fusion.22
  16.7 1.7 copy.28.embed_out
  18.4 204.0 %shard_map.184 = (f32[8,8,384]{2,1,0:T(8,128)}, bf16[8,128,1152]{2,1,0:T(8,128)(2,1)}, f32[8,16,128]{2,1,0:T(8,128)}) custom-call(bf16[144,2304]{1,0:T(8,128)(2,1)} %bitcast.90, bf16[288,1152]{1,0:T(8,128)(2,1)} %bitcast.91, f32[8,384]{1,0:T(8,128)} %select_maximum_fusion.packed_in, bf16[128,1152]{1,0:T(8,128)(2,1)} %bitcast.89, bf16[1152,1152]{1,0:T(8,128)(2,1)} %stud_up.1, ...), custom_call_target="tpu_custom_call" | custom-call | tf_op jit(solution)/shard_map/pallas_call | solution.py:388
  222.4 1.0 and_reduce_fusion
  223.4 0.9 fusion.46
  224.3 1.2 multiply_reduce_fusion.2
  225.5 0.8 slice.94
  228.3 1.0 copy.29
  230.3 0.8 slice_bitcast_fusion
  231.1 2.8 %fusion.13 = (f32[64,16]{1,0:T(8,128)S(1)}, bf16[64,16,1152]{2,1,0:T(8,128)(2,1)S(1)}) fusion(bf16[64,16,1152]{2,1,0:T(8,128)(2,1)} %bitcast.77, f32[64,1152]{1,0:T(8,128)S(1)} %get-tuple-element.25, bf16[64,16,16]{2,1,0:T(8,128)(2,1)S(1)} %copy.31, bf16[16,1152]{1,0:T(8,128)(2,1)S(1)} %copy-done.8), kind=kOutput, calls=%fused_computation.28 | convolution fusion | flops 44825600 | bytes 5087232 | tf_op jit(solution)/shard_map/dot_general | solution.py:50
  233.8 2.8 %multiply_reduce_fusion.1 = f32[64,16]{1,0:T(8,128)S(1)} fusion(f32[64,16]{1,0:T(8,128)S(1)} %broadcast_multiply_fusion, bf16[64,16,1152]{2,1,0:T(8,128)(2,1)} %bitcast.78, f32[64,1152]{1,0:T(8,128)S(1)} %get-tuple-element.25, bf16[64,16,1152]{2,1,0:T(8,128)(2,1)S(1)} %get-tuple-element.58), kind=kLoop, calls=%fused_computation.25 | loop fusion | flops 8256512 | bytes 5021696 | tf_op jit(solution)/shard_map/jvp()/reduce_sum | solution.py:31
  236.7 1.2 multiply_convert_fusion.1
  237.9 0.7 fusion.60
  238.7 0.9 reshape.280
  239.5 1.0 subtract_multiply_fusion
  240.5 0.8 copy.33
  241.3 1.2 copy.34
  242.5 4.9 %multiply_reduce_fusion = (f32[64,16]{1,0:T(8,128)S(1)}, f32[64,16]{1,0:T(8,128)S(1)}, f32[64,16,1152]{2,1,0:T(8,128)S(1)}) fusion(f32[64,16]{1,0:T(8,128)S(1)} %broadcast_multiply_fusion, bf16[64,16,1152]{2,1,0:T(8,128)(2,1)} %bitcast.79, f32[64,1152]{1,0:T(8,128)S(1)} %get-tuple-element.25, bf16[64,16,1152]{2,1,0:T(8,128)(2,1)S(1)} %get-tuple-element.58, ...), kind=kOutput, calls=%fused_computation.23 | convolution fusion | flops 235927552 | bytes 9846784 | tf_op jit(solution)/shard_map/dot_general | solution.py:569
  247.4 2.8 %fusion.26 = (f32[64,16]{1,0:T(8,128)S(1)}, f32[64,16]{1,0:T(8,128)S(1)}) fusion(f32[64,16]{1,0:T(8,128)S(1)} %multiply_multiply_fusion.2, f32[64,16]{1,0:T(8,128)S(1)} %broadcast_multiply_fusion, bf16[64,16,1152]{2,1,0:T(8,128)(2,1)S(1)} %bitcast.81, f32[64,1152]{1,0:T(8,128)S(1)} %get-tuple-element.25, bf16[64,16,1152]{2,1,0:T(8,128)(2,1)S(1)} %get-tuple-element.58, ...), kind=kLoop, calls=%fused_computation.47 | loop fusion | flops 15333376 | bytes 9756672 | tf_op jit(solution)/shard_map/transpose(jvp())/reduce_sum | solution.py:30
  250.3 4.2 %multiply_convert_fusion = (bf16[64,16,1152]{2,1,0:T(8,128)(2,1)}, bf16[64,16,1152]{2,1,0:T(8,128)(2,1)S(1)}) fusion(f32[64,16]{1,0:T(8,128)S(1)} %negate_multiply_fusion, f32[64,1152]{1,0:T(8,128)S(1)} %get-tuple-element.25, f32[64,16]{1,0:T(8,128)S(1)} %multiply_multiply_fusion.2, f32[64,16]{1,0:T(8,128)S(1)} %broadcast_multiply_fusion, ...), kind=kLoop, calls=%fused_computation.22 | loop fusion | flops 20054016 | bytes 15065088 | tf_op jit(solution)/shard_map/convert_element_type | solution.py:575
  254.5 6.0 %add_multiply_fusion = (f32[1024,1152]{1,0:T(8,128)}, f32[1024,1152]{1,0:T(8,128)}) fusion(bf16[1024,1152]{1,0:T(8,128)(2,1)S(1)} %bitcast.87, bf16[1152,1152]{1,0:T(8,128)(2,1)S(1)} %copy-done.4), kind=kOutput, calls=%fused_computation.26 | convolution fusion | flops 2726166528 | bytes 14450688 | tf_op jit(solution)/shard_map/dot_general | solution.py:490
  260.5 9.5 %fusion.15 = f32[144,1152]{1,0:T(8,128)} fusion(f32[1024,1152]{1,0:T(8,128)} %get-tuple-element.61, bf16[1024,1152]{1,0:T(8,128)(2,1)S(1)} %bitcast.84, bf16[1152,1152]{1,0:T(8,128)(2,1)} %stud_down.1, bf16[1024,1152]{1,0:T(8,128)(2,1)} %bitcast.88, s32[]{:T(128)S(6)} %select_n.32), kind=kOutput, calls=%fused_computation.32 | convolution fusion | flops 3080060928 | bytes 10919940 | tf_op jit(solution)/shard_map/dot_general | solution.py:584
  270.0 4.0 %fusion.23 = f32[144,1152]{1,0:T(8,128)} fusion(bf16[1024,1152]{1,0:T(8,128)(2,1)S(1)} %bitcast.85, f32[1024,1152]{1,0:T(8,128)} %get-tuple-element.60, s32[]{:T(128)S(6)} %select_n.32, f32[1024,1152]{1,0:T(8,128)} %get-tuple-element.61), kind=kOutput, calls=%fused_computation.44 | convolution fusion | flops 340033536 | bytes 5120004 | tf_op jit(solution)/shard_map/dot_general | solution.py:587
  (72 shorter events, 8.9 us)
Async XLA Ops:
  15.4 2.9 %copy-start.3 = (bf16[8,16,1152]{2,1,0:T(8,128)(2,1)}, bf16[8,16,1152]{2,1,0:T(8,128)(2,1)S(1)}, u32[]{:S(2)}) copy-start(bf16[8,16,1152]{2,1,0:T(8,128)(2,1)S(1)} %get-tuple-element.56) | copy-start | bytes 884740
  15.7 210.8 %copy-start.7 = (bf16[1001,1152]{1,0:T(8,128)(2,1)S(1)}, bf16[1001,1152]{1,0:T(8,128)(2,1)}, u32[]{:S(2)}) copy-start(bf16[1001,1152]{1,0:T(8,128)(2,1)} %param.24) | copy-start | bytes 6918916
  18.3 209.8 %copy-start.15 = (f32[1152]{0:T(1024)S(1)}, f32[1152]{0:T(1024)}, u32[]{:S(2)}) copy-start(f32[1152]{0:T(1024)} %param.35) | copy-start | bytes 13828
  18.3 211.9 %copy-start.13 = (f32[3,1152]{1,0:T(4,128)S(1)}, f32[3,1152]{1,0:T(4,128)}, u32[]{:S(2)}) copy-start(f32[3,1152]{1,0:T(4,128)} %param.34) | copy-start | bytes 41476
  18.3 211.9 %copy-start.14 = (f32[3,1152]{1,0:T(4,128)S(1)}, f32[3,1152]{1,0:T(4,128)}, u32[]{:S(2)}) copy-start(f32[3,1152]{1,0:T(4,128)} %param.33) | copy-start | bytes 41476
  222.4 8.7 %copy-start.8 = (bf16[16,1152]{1,0:T(8,128)(2,1)S(1)}, bf16[16,1152]{1,0:T(8,128)(2,1)}, u32[]{:S(2)}) copy-start(bf16[16,1152]{1,0:T(8,128)(2,1)} %embed_in.1) | copy-start | bytes 110596
  229.6 1.5 copy-start.10
  231.1 5.7 %copy-start = (bf16[8,128,1152]{2,1,0:T(8,128)(2,1)S(1)}, bf16[8,128,1152]{2,1,0:T(8,128)(2,1)}, u32[]{:S(2)}) copy-start(bf16[8,128,1152]{2,1,0:T(8,128)(2,1)} %get-tuple-element.9) | copy-start | bytes 7077892
  236.7 1.2 copy-start.11
  236.7 1.2 copy-start.9
  242.4 4.9 %copy-start.12 = (f32[64,16]{1,0:T(8,128)S(1)}, f32[64,16]{1,0:T(8,128)}, u32[]{:S(2)}) copy-start(f32[64,16]{1,0:T(8,128)} %copy-done.11) | copy-start | bytes 12292
  242.5 5.0 %copy-start.1 = (bf16[8,128,1152]{2,1,0:T(8,128)(2,1)S(1)}, bf16[8,128,1152]{2,1,0:T(8,128)(2,1)}, u32[]{:S(2)}) copy-start(bf16[8,128,1152]{2,1,0:T(8,128)(2,1)} %get-tuple-element.9) | copy-start | bytes 7077892
  247.4 2.8 %copy-start.6 = (f32[64,1152]{1,0:T(8,128)S(1)}, f32[64,1152]{1,0:T(8,128)}, u32[]{:S(2)}) copy-start(f32[64,1152]{1,0:T(8,128)} %get-tuple-element.27) | copy-start | bytes 884740
  250.2 4.2 %copy-start.4 = (bf16[1152,1152]{1,0:T(8,128)(2,1)S(1)}, bf16[1152,1152]{1,0:T(8,128)(2,1)}, u32[]{:S(2)}) copy-start(bf16[1152,1152]{1,0:T(8,128)(2,1)} %stud_up.1) | copy-start | bytes 7962628
  254.5 6.0 %copy-start.5 = (bf16[64,16,1152]{2,1,0:T(8,128)(2,1)}, bf16[64,16,1152]{2,1,0:T(8,128)(2,1)S(1)}, u32[]{:S(2)}) copy-start(bf16[64,16,1152]{2,1,0:T(8,128)(2,1)S(1)} %get-tuple-element.24) | copy-start | bytes 7077892
  254.5 6.0 %copy-start.2 = (bf16[64,16,1152]{2,1,0:T(8,128)(2,1)S(1)}, bf16[64,16,1152]{2,1,0:T(8,128)(2,1)}, u32[]{:S(2)}) copy-start(bf16[64,16,1152]{2,1,0:T(8,128)(2,1)} %get-tuple-element.23) | copy-start | bytes 7077892
